TPU v7x, 8 devices: a whole 2x2x1 slice. The times are simulated.
8 devices in a mesh: dp: 2 (over z, y), tp: 4 (over x, core).
Axes of the slice: x: 2, y: 2, z: 1, core: 2. Of those that a mesh axis runs over, the one named last changes fastest.
Arguments:
- residual: bfloat16 [512, 4096], P('dp'), parts along dimension 0
- positions: int32 [512], P('dp'), parts along dimension 0
- k_cache: bfloat16 [2, 512, 8, 64, 128], P(None, 'dp', 'tp'), parts along dimension 1
- v_cache: bfloat16 [2, 512, 8, 64, 128], P(None, 'dp', 'tp'), parts along dimension 1
- ln_weight: bfloat16 [2, 4096], replicated
- w_q: bfloat16 [2, 4096, 4096], P(None, None, 'tp')
- w_k: bfloat16 [2, 4096, 1024], P(None, None, 'tp')
- w_v: bfloat16 [2, 4096, 1024], P(None, None, 'tp')
- q_norm_w: bfloat16 [2, 32, 128], P(None, 'tp')
- k_norm_w: bfloat16 [2, 8, 128], P(None, 'tp')
- w_o: bfloat16 [2, 4096, 4096], P(None, 'tp')
- w_gate: bfloat16 [2, 4096, 14336], P(None, None, 'tp')
- w_up: bfloat16 [2, 4096, 14336], P(None, None, 'tp')
- w_down: bfloat16 [2, 14336, 4096], P(None, 'tp')
Outputs:
- output 1: bfloat16 [512, 4096], P('dp'), parts along dimension 0
- output 2: bfloat16 [2, 512, 8, 64, 128], P(None, 'dp', 'tp'), parts along dimension 1
- output 3: bfloat16 [2, 512, 8, 64, 128], P(None, 'dp', 'tp'), parts along dimension 1
There are 2 independent parts. A program takes and returns all parts, laid end to end along the dimension named above; an argument that names none is the same for every part.
All inputs are finite; a program needn't handle non-finite values.
Results may differ from a plain program's by a relative error of at most 0.016126.
Values are sent between devices in bfloat16 or wider.
A program may use at most 1.25 GiB of HBM per device.

v0:
```python
import math
import jax
import jax.numpy as jnp
from jax import lax
from jax.sharding import PartitionSpec as P, NamedSharding

EPS = 1e-5
ROPE_THETA = 75000000.0


def cohere_norm(values, weight):
    centered = values - jnp.mean(values, axis=-1, keepdims=True)
    variance = jnp.mean(centered * centered, axis=-1, keepdims=True)
    return centered * lax.rsqrt(variance + EPS) * weight.astype(jnp.float32)


def rotate(values, cos_t, sin_t):
    paired = values.reshape(values.shape[:-1] + (values.shape[-1] // 2, 2))
    even_part = paired[..., 0]
    odd_part = paired[..., 1]
    turned = jnp.stack([even_part * cos_t - odd_part * sin_t, odd_part * cos_t + even_part * sin_t], axis=-1)
    return turned.reshape(values.shape)


def rope_tables(positions, head_dim):
    half_ids = jnp.arange(head_dim // 2, dtype=jnp.float32)
    inv_freq = ROPE_THETA ** (-2.0 * half_ids / head_dim)
    angles = positions.astype(jnp.float32)[:, None] * inv_freq[None, :]
    return jnp.cos(angles)[:, None, :], jnp.sin(angles)[:, None, :]


def project_heads(hidden, weight, norm_w, cos_t, sin_t):
    projected = jnp.dot(hidden, weight, preferred_element_type=jnp.float32).astype(jnp.bfloat16)
    per_head = projected.reshape(hidden.shape[0], norm_w.shape[0], norm_w.shape[1]).astype(jnp.float32)
    return rotate(cohere_norm(per_head, norm_w), cos_t, sin_t).astype(jnp.bfloat16)


def attend(q_rot, k_new, v_new, k_old, v_old, positions):
    row_count, kv_local, seq_len, head_dim = k_old.shape
    q_grouped = q_rot.reshape(row_count, kv_local, -1, head_dim)
    score_scale = 1.0 / math.sqrt(head_dim)
    old_scores = jnp.einsum("bkgd,bksd->bkgs", q_grouped, k_old, preferred_element_type=jnp.float32) * score_scale
    earlier = jnp.arange(seq_len)[None, None, None, :] < positions[:, None, None, None]
    old_scores = jnp.where(earlier, old_scores, -1e30)
    new_score = jnp.einsum("clhe,cle->clh", q_grouped, k_new, preferred_element_type=jnp.float32) * score_scale
    row_max = jnp.maximum(jnp.max(old_scores, axis=-1), new_score)
    old_exp = jnp.exp(old_scores - row_max[..., None])
    new_exp = jnp.exp(new_score - row_max)
    denominator = jnp.sum(old_exp, axis=-1) + new_exp
    old_prob = (old_exp / denominator[..., None]).astype(jnp.bfloat16)
    new_prob = (new_exp / denominator).astype(jnp.bfloat16)
    attn_mix = jnp.einsum("bkgs,bksd->bkgd", old_prob, v_old, preferred_element_type=jnp.float32)
    attn_mix = attn_mix + new_prob.astype(jnp.float32)[..., None] * v_new.astype(jnp.float32)[:, :, None, :]
    return attn_mix.astype(jnp.bfloat16).reshape(row_count, -1)


def mlp_partial(hidden, gate_w, up_w, down_w):
    gate_proj = jnp.dot(hidden, gate_w, preferred_element_type=jnp.float32).astype(jnp.bfloat16)
    up_proj = jnp.dot(hidden, up_w, preferred_element_type=jnp.float32).astype(jnp.bfloat16)
    activated = (jax.nn.silu(gate_proj.astype(jnp.float32)) * up_proj.astype(jnp.float32)).astype(jnp.bfloat16)
    return jnp.dot(activated, down_w, preferred_element_type=jnp.float32)


def write_caches(k_cache, v_cache, new_keys, new_values, positions):
    seq_len = k_cache.shape[3]
    at_pos = jnp.arange(seq_len)[None, None, None, :, None] == positions[None, :, None, None, None]
    k_out = jnp.where(at_pos, jnp.stack(new_keys)[:, :, :, None, :], k_cache)
    v_out = jnp.where(at_pos, jnp.stack(new_values)[:, :, :, None, :], v_cache)
    return k_out, v_out


def solution(mesh):
    cache_spec = P(None, "dp", "tp", None, None)
    col_spec = P(None, None, "tp")
    row_spec = P(None, "tp", None)
    resid_spec = P("dp", None)
    in_specs = (resid_spec, P("dp"), cache_spec, cache_spec, P(None, None), col_spec, col_spec, col_spec, row_spec, row_spec, row_spec, col_spec, col_spec, row_spec)
    out_specs = (resid_spec, cache_spec, cache_spec)

    def local_step(residual, positions, k_cache, v_cache, ln_weight, w_q, w_k, w_v, q_norm_w, k_norm_w, w_o, w_gate, w_up, w_down):
        cos_t, sin_t = rope_tables(positions, k_cache.shape[4])
        resid_x = residual
        new_keys = []
        new_values = []
        for layer_idx in range(k_cache.shape[0]):
            hidden = cohere_norm(resid_x.astype(jnp.float32), ln_weight[layer_idx]).astype(jnp.bfloat16)
            q_rot = project_heads(hidden, w_q[layer_idx], q_norm_w[layer_idx], cos_t, sin_t)
            k_rot = project_heads(hidden, w_k[layer_idx], k_norm_w[layer_idx], cos_t, sin_t)
            v_proj = jnp.dot(hidden, w_v[layer_idx], preferred_element_type=jnp.float32).astype(jnp.bfloat16).reshape(k_rot.shape)
            attn_heads = attend(q_rot, k_rot, v_proj, k_cache[layer_idx], v_cache[layer_idx], positions)
            attn_part = jnp.dot(attn_heads, w_o[layer_idx], preferred_element_type=jnp.float32).astype(jnp.bfloat16)
            attn_sum = lax.psum(attn_part, "tp")
            mlp_part = mlp_partial(hidden, w_gate[layer_idx], w_up[layer_idx], w_down[layer_idx]).astype(jnp.bfloat16)
            mlp_sum = lax.psum(mlp_part, "tp")
            resid_x = (resid_x.astype(jnp.float32) + attn_sum.astype(jnp.float32) + mlp_sum.astype(jnp.float32)).astype(jnp.bfloat16)
            new_keys.append(k_rot)
            new_values.append(v_proj)
        k_out, v_out = write_caches(k_cache, v_cache, new_keys, new_values, positions)
        return resid_x, k_out, v_out

    return jax.shard_map(local_step, mesh=mesh, in_specs=in_specs, out_specs=out_specs, check_vma=False)
```

profile of v0, /device:TPU:0, one launch (start us, length us, event | category | flops | bytes accessed | tf_op | source)
XLA Modules:
  0.0 390.0 jit_solution(925433087115815184)
XLA Ops:
  7.3 0.8 convert_element_type.248
  8.1 1.4 iota_compare_fusion
  9.5 2.0 convert_reduce_fusion.1
  11.5 2.3 fusion.97
  13.8 0.6 slice_convert_fusion.4
  14.4 0.6 slice_convert_fusion.2
  14.9 0.6 slice_convert_fusion
  15.8 1.1 copy.132
  16.9 2.8 fusion.152
  19.8 0.8 copy.141
  20.6 2.8 bitcast_reduce_fusion.1
  24.7 0.7 copy.169
  25.4 5.8 %fusion.137 = f32[256,1024]{1,0:T(8,128)S(1)} fusion(bf16[2,4096,1024]{2,1,0:T(8,128)(2,1)} %param.19, bf16[256,4096]{1,0:T(8,128)(2,1)S(1)} %copy-done, f32[4096]{0:T(1024)S(1)} %bitcast.229, f32[256]{0:T(256)S(1)} %add_rsqrt_fusion.5, f32[256]{0:T(256)S(1)} %broadcast_multiply_fusion.5), kind=kOutput, calls=%fused_computation.99 | convolution fusion | flops 2153250816 | bytes 11552768 | tf_op jit(solution)/shard_map/dot_general | solution.py:33
  31.2 1.3 copy.127
  32.5 1.4 copy.171
  34.4 0.8 copy.129
  35.2 1.5 multiply_reduce_fusion.3
  36.8 1.9 reshape.281
  38.7 1.8 multiply_multiply_fusion.1
  40.5 1.4 subtract_convert_fusion.1
  41.9 1.2 pad_maximum_fusion
  43.3 1.1 copy.133
  44.4 1.1 multiply_reduce_fusion.1
  45.5 9.0 %fusion.207 = (f32[256,2,4]{2,1,0:T(2,128)}, f32[256,2,4,64]{3,2,1,0:T(4,128)S(1)}) fusion(bf16[256,2,4,128]{3,2,1,0:T(4,128)(2,1)} %copy.133, bf16[2,256,2,64,128]{4,3,2,1,0:T(8,128)(2,1)} %param.16, pred[256,64]{1,0:T(8,128)(4,1)S(1)} %copy-done.11), kind=kOutput, calls=%fused_computation.189 | convolution fusion | flops 33945600 | bytes 9461760 | tf_op jit(solution)/shard_map/bkgd,bksd->bkgs/dot_general | solution.py:42
  54.4 1.1 copy.136
  55.5 0.9 copy.137
  56.3 3.0 fusion.170
  59.4 1.1 copy.138
  60.5 0.9 copy.139
  61.3 0.9 copy.140
  62.2 5.8 %fusion.131 = bf16[256,2,4,128]{3,2,1,0:T(4,128)(2,1)} fusion(bf16[2,256,2,64,128]{4,3,2,1,0:T(8,128)(2,1)} %param.17, f32[256,2,4,64]{3,2,1,0:T(4,128)S(1)} %get-tuple-element.34, f32[256,2,128]{2,1,0:T(2,128)} %copy.141, f32[256,2,4]{2,1,0:T(2,128)} %copy.140, f32[256,2,4]{2,1,0:T(2,128)} %copy.139, f32[256,2,4]{2,1,0:T(2,128)} %copy.137), kind=kOutput, calls=%fused_computation.97 | convolution fusion | flops 34734080 | bytes 10485760 | tf_op jit(solution)/shard_map/bkgs,bksd->bkgd/dot_general | solution.py:52
  68.0 1.4 reshape.278
  69.5 15.1 %fusion.51 = f32[256,3584]{1,0:T(8,128)} fusion(bf16[2,4096,3584]{2,1,0:T(8,128)(2,1)} %param.25, bf16[256,4096]{1,0:T(8,128)(2,1)S(1)} %copy-done, f32[4096]{0:T(1024)S(1)} %bitcast.230, f32[256]{0:T(256)S(1)} %copy-done.25, f32[256]{0:T(256)S(1)} %copy-done.18), kind=kOutput, calls=%fused_computation.53 | convolution fusion | flops 7523270656 | bytes 35145728 | tf_op jit(solution)/shard_map/dot_general | solution.py:58
  84.6 7.0 %fusion.42 = bf16[256,4096]{1,0:T(8,128)(2,1)} fusion(bf16[256,1024]{1,0:T(8,128)(2,1)S(1)} %reshape.278, bf16[2,1024,4096]{2,1,0:T(8,128)(2,1)} %param.24), kind=kOutput, calls=%fused_computation.50 | convolution fusion | flops 2148532224 | bytes 11010048 | tf_op jit(solution)/shard_map/dot_general | solution.py:91
  91.6 15.5 %fusion.63.clone.5 = bf16[256,3584]{1,0:T(8,128)(2,1)} fusion(bf16[2,4096,3584]{2,1,0:T(8,128)(2,1)} %param.26, f32[256,3584]{1,0:T(8,128)} %fusion.51, bf16[256,4096]{1,0:T(8,128)(2,1)S(1)} %copy-done, f32[4096]{0:T(1024)S(1)} %bitcast.231, f32[256]{0:T(256)S(1)} %copy-done.25, f32[256]{0:T(256)S(1)} %copy-done.18), kind=kOutput, calls=%fused_computation.57.clone.clone.clone.2 | convolution fusion | flops 7528775680 | bytes 36980736 | tf_op jit(solution)/shard_map/dot_general | solution.py:59
  107.2 14.8 %fusion.66 = bf16[256,4096]{1,0:T(8,128)(2,1)} fusion(bf16[2,3584,4096]{2,1,0:T(8,128)(2,1)} %param.27, bf16[256,3584]{1,0:T(8,128)(2,1)} %fusion.63.clone.5), kind=kOutput, calls=%fused_computation.58 | convolution fusion | flops 7517241344 | bytes 33292288 | tf_op jit(solution)/shard_map/dot_general | solution.py:61
  122.2 0.4 copy-done.12
  122.9 1.1 copy.147
  124.0 80.7 %all-reduce.7.cloned.1.call-done = (bf16[256,4096]{1,0:T(8,128)(2,1)}, bf16[256,4096]{1,0:T(8,128)(2,1)}) async-done(((bf16[256,4096]{1,0:T(8,128)(2,1)}, bf16[256,4096]{1,0:T(8,128)(2,1)}), (bf16[256,4096]{1,0:T(8,128)(2,1)}, bf16[256,4096]{1,0:T(8,128)(2,1)})) %all-reduce.7.cloned.1.call-update) | async-done | bytes 4194320 | tf_op jit(solution)/shard_map/psum | solution.py:94
  204.7 3.5 convert_reduce_fusion
  208.2 0.7 fusion.94
  209.0 1.3 fusion.161
  210.3 0.8 copy-done.29
  211.1 1.3 bitcast_reduce_fusion
  212.4 5.8 %fusion.143 = f32[256,1024]{1,0:T(8,128)S(1)} fusion(bf16[2,4096,1024]{2,1,0:T(8,128)(2,1)} %param.19, bf16[256,4096]{1,0:T(8,128)(2,1)S(1)} %get-tuple-element.8, f32[4096]{0:T(1024)S(1)} %bitcast.224, f32[256]{0:T(256)S(1)} %add_rsqrt_fusion.4, f32[256]{0:T(256)S(1)} %broadcast_multiply_fusion.4), kind=kOutput, calls=%fused_computation.101 | convolution fusion | flops 2153250816 | bytes 11552768 | tf_op jit(solution)/shard_map/dot_general | solution.py:33
  218.3 14.8 %fusion.72 = f32[256,3584]{1,0:T(8,128)} fusion(bf16[2,4096,3584]{2,1,0:T(8,128)(2,1)} %param.25, bf16[256,4096]{1,0:T(8,128)(2,1)S(1)} %get-tuple-element.8, f32[4096]{0:T(1024)S(1)} %bitcast.225, f32[256]{0:T(256)S(1)} %add_rsqrt_fusion.4, f32[256]{0:T(256)S(1)} %broadcast_multiply_fusion.4), kind=kOutput, calls=%fused_computation.60 | convolution fusion | flops 7523270656 | bytes 35145728 | tf_op jit(solution)/shard_map/dot_general | solution.py:58
  233.1 0.9 copy.158
  234.0 0.8 copy.156
  236.4 0.7 copy.170
  238.3 0.6 multiply_reduce_fusion.2
  239.0 0.6 reshape.289
  239.6 1.8 multiply_multiply_fusion
  241.5 1.4 subtract_convert_fusion
  242.8 1.2 pad_maximum_fusion.1
  244.7 8.1 %fusion.208 = (f32[256,2,4]{2,1,0:T(2,128)S(1)}, f32[256,2,4,64]{3,2,1,0:T(4,128)S(1)}) fusion(bf16[256,2,4,128]{3,2,1,0:T(4,128)(2,1)S(1)} %copy.148, bf16[2,256,2,64,128]{4,3,2,1,0:T(8,128)(2,1)} %param.16, pred[256,64]{1,0:T(8,128)(4,1)} %get-tuple-element.30), kind=kOutput, calls=%fused_computation.190 | convolution fusion | flops 33945600 | bytes 9478144 | tf_op jit(solution)/shard_map/bkgd,bksd->bkgs/dot_general | solution.py:42
  253.1 1.4 fusion.171
  255.1 4.8 %fusion.128 = bf16[256,2,4,128]{3,2,1,0:T(4,128)(2,1)S(1)} fusion(bf16[2,256,2,64,128]{4,3,2,1,0:T(8,128)(2,1)} %param.17, f32[256,2,4,64]{3,2,1,0:T(4,128)S(1)} %get-tuple-element.38, f32[256,2,128]{2,1,0:T(2,128)S(1)} %copy-done.8, f32[256,2,4]{2,1,0:T(2,128)S(1)} %copy.155, f32[256,2,4]{2,1,0:T(2,128)S(1)} %copy.154, f32[256,2,4]{2,1,0:T(2,128)S(1)} %copy.152), kind=kOutput, calls=%fused_computation.96 | convolution fusion | flops 34734080 | bytes 9723904 | tf_op jit(solution)/shard_map/bkgs,bksd->bkgd/dot_general | solution.py:52
  260.3 7.2 %fusion.45 = bf16[256,4096]{1,0:T(8,128)(2,1)} fusion(bf16[256,1024]{1,0:T(8,128)(2,1)S(1)} %reshape.279, bf16[2,1024,4096]{2,1,0:T(8,128)(2,1)} %param.24), kind=kOutput, calls=%fused_computation.51 | convolution fusion | flops 2148532224 | bytes 11010048 | tf_op jit(solution)/shard_map/dot_general | solution.py:91
  267.5 15.7 %fusion.84.clone.5 = bf16[256,3584]{1,0:T(8,128)(2,1)} fusion(bf16[2,4096,3584]{2,1,0:T(8,128)(2,1)} %param.26, f32[256,3584]{1,0:T(8,128)} %fusion.72, bf16[256,4096]{1,0:T(8,128)(2,1)S(1)} %copy-done.2, f32[4096]{0:T(1024)S(1)} %bitcast.226, f32[256]{0:T(256)S(1)} %copy-done.27, f32[256]{0:T(256)S(1)} %copy-done.20), kind=kOutput, calls=%fused_computation.64.clone.clone.clone.2 | convolution fusion | flops 7528775680 | bytes 36980736 | tf_op jit(solution)/shard_map/dot_general | solution.py:59
  283.1 14.8 %fusion.87 = bf16[256,4096]{1,0:T(8,128)(2,1)} fusion(bf16[2,3584,4096]{2,1,0:T(8,128)(2,1)} %param.27, bf16[256,3584]{1,0:T(8,128)(2,1)} %fusion.84.clone.5), kind=kOutput, calls=%fused_computation.65 | convolution fusion | flops 7517241344 | bytes 33292288 | tf_op jit(solution)/shard_map/dot_general | solution.py:61
  298.0 0.9 copy-done.4
  298.9 23.3 %broadcast_select_fusion = (bf16[2,256,2,64,128]{4,3,2,1,0:T(8,128)(2,1)}, bf16[2,256,2,64,128]{4,3,2,1,0:T(8,128)(2,1)}) fusion(bf16[2,256,2,64,128]{4,3,2,1,0:T(8,128)(2,1)} %param.17, pred[256,64]{1,0:T(8,128)(4,1)S(1)} %copy-done.9, bf16[2,256,2,128]{3,2,1,0:T(2,128)(2,1)S(1)} %copy-done.4, bf16[2,256,2,64,128]{4,3,2,1,0:T(8,128)(2,1)} %param.16, ...), kind=kLoop, calls=%fused_computation.18 | loop fusion | flops 16777216 | bytes 67649536 | tf_op jit(solution)/shard_map/jit(_where)/select_n | solution.py:68
  322.2 55.8 %all-reduce.5.cloned.1.call-done = (bf16[256,4096]{1,0:T(8,128)(2,1)}, bf16[256,4096]{1,0:T(8,128)(2,1)}) async-done(((bf16[256,4096]{1,0:T(8,128)(2,1)}, bf16[256,4096]{1,0:T(8,128)(2,1)}), (bf16[256,4096]{1,0:T(8,128)(2,1)}, bf16[256,4096]{1,0:T(8,128)(2,1)})) %all-reduce.5.cloned.1.call-update) | async-done | bytes 4194320 | tf_op jit(solution)/shard_map/psum | solution.py:94
  378.0 4.7 %fusion.103 = bf16[256,4096]{1,0:T(8,128)(2,1)} fusion(bf16[256,4096]{1,0:T(8,128)(2,1)S(1)} %copy-done.2, bf16[256,4096]{1,0:T(8,128)(2,1)} %get-tuple-element.3, bf16[256,4096]{1,0:T(8,128)(2,1)} %get-tuple-element.4), kind=kLoop, calls=%fused_computation.79 | loop fusion | flops 6291456 | bytes 8388608 | tf_op jit(solution)/shard_map/convert_element_type | solution.py:95
  (117 shorter events, 7.3 us)
Async XLA Ops:
  7.2 9.8 %copy-start = (bf16[256,4096]{1,0:T(8,128)(2,1)S(1)}, bf16[256,4096]{1,0:T(8,128)(2,1)}, u32[]{:S(2)}) copy-start(bf16[256,4096]{1,0:T(8,128)(2,1)} %param.14) | copy-start | bytes 6291460
  7.2 6.6 %copy-start.23 = (bf16[2,2,128]{2,1,0:T(2,128)(2,1)S(1)}, bf16[2,2,128]{2,1,0:T(2,128)(2,1)}, u32[]{:S(2)}) copy-start(bf16[2,2,128]{2,1,0:T(2,128)(2,1)} %param.23) | copy-start | bytes 3076
  7.2 7.2 %copy-start.22 = (bf16[2,8,128]{2,1,0:T(8,128)(2,1)S(1)}, bf16[2,8,128]{2,1,0:T(8,128)(2,1)}, u32[]{:S(2)}) copy-start(bf16[2,8,128]{2,1,0:T(8,128)(2,1)} %param.22) | copy-start | bytes 12292
  7.2 7.7 %copy-start.10 = (bf16[2,4096]{1,0:T(2,128)(2,1)S(1)}, bf16[2,4096]{1,0:T(2,128)(2,1)}, u32[]{:S(2)}) copy-start(bf16[2,4096]{1,0:T(2,128)(2,1)} %param.18) | copy-start | bytes 49156
  7.2 197.5 %all-reduce.7.cloned.1.call-start = ((), (), s32[]{:S(2)}) async-start(), calls=%async_computation.1 | async-start | bytes 8388608 | tf_op jit(solution)/shard_map/psum | solution.py:94
  11.4 14.0 %copy-start.17 = (f32[256]{0:T(256)}, f32[256]{0:T(256)S(1)}, u32[]{:S(2)}) copy-start(f32[256]{0:T(256)S(1)} %broadcast_multiply_fusion.5) | copy-start | bytes 3076
  13.8 11.7 %copy-start.24 = (f32[256]{0:T(256)}, f32[256]{0:T(256)S(1)}, u32[]{:S(2)}) copy-start(f32[256]{0:T(256)S(1)} %add_rsqrt_fusion.5) | copy-start | bytes 3076
  15.6 9.9 %copy-start.15 = (f32[1,4096]{1,0:T(1,128)}, f32[1,4096]{1,0:T(1,128)S(1)}, u32[]{:S(2)}) copy-start(f32[1,4096]{1,0:T(1,128)S(1)} %get-tuple-element.24) | copy-start | bytes 49156
  19.8 3.7 copy-start.6
  31.2 1.3 copy-start.3
  38.7 6.8 %copy-start.11 = (pred[256,64]{1,0:T(8,128)(4,1)S(1)}, pred[256,64]{1,0:T(8,128)(4,1)}, u32[]{:S(2)}) copy-start(pred[256,64]{1,0:T(8,128)(4,1)} %get-tuple-element.30) | copy-start | bytes 49156
  62.2 7.2 %copy-start.16 = (f32[1,4096]{1,0:T(1,128)S(1)}, f32[1,4096]{1,0:T(1,128)}, u32[]{:S(2)}) copy-start(f32[1,4096]{1,0:T(1,128)} %copy-done.15) | copy-start | bytes 49156
  62.2 7.3 %copy-start.18 = (f32[256]{0:T(256)S(1)}, f32[256]{0:T(256)}, u32[]{:S(2)}) copy-start(f32[256]{0:T(256)} %copy-done.17) | copy-start | bytes 3076
  62.2 7.3 %copy-start.25 = (f32[256]{0:T(256)S(1)}, f32[256]{0:T(256)}, u32[]{:S(2)}) copy-start(f32[256]{0:T(256)} %copy-done.24) | copy-start | bytes 3076
  122.0 0.7 copy-start.12
  122.0 0.8 copy-start.21
  122.0 256.0 %all-reduce.5.cloned.1.call-start = ((), (), s32[]{:S(2)}) async-start(), calls=%async_computation | async-start | bytes 8388608 | tf_op jit(solution)/shard_map/psum | solution.py:94
  204.7 4.2 %copy-start.13 = (f32[1,4096]{1,0:T(1,128)S(1)}, f32[1,4096]{1,0:T(1,128)}, u32[]{:S(2)}) copy-start(f32[1,4096]{1,0:T(1,128)} %get-tuple-element.23) | copy-start | bytes 49156
  204.7 4.2 %copy-start.28 = (bf16[2,4096,256]{2,1,0:T(8,128)(2,1)S(1)}, bf16[2,4096,256]{2,1,0:T(8,128)(2,1)}, u32[]{:S(2)}) copy-start(bf16[2,4096,256]{2,1,0:T(8,128)(2,1)} %param.21) | copy-start | bytes 12582916
  208.2 10.0 %copy-start.1 = (bf16[256,4096]{1,0:T(8,128)(2,1)}, bf16[256,4096]{1,0:T(8,128)(2,1)S(1)}, u32[]{:S(2)}) copy-start(bf16[256,4096]{1,0:T(8,128)(2,1)S(1)} %get-tuple-element.8) | copy-start | bytes 6291460
  208.2 10.0 %copy-start.19 = (f32[256]{0:T(256)}, f32[256]{0:T(256)S(1)}, u32[]{:S(2)}) copy-start(f32[256]{0:T(256)S(1)} %broadcast_multiply_fusion.4) | copy-start | bytes 3076
  208.9 2.2 copy-start.29
  209.0 9.3 %copy-start.26 = (f32[256]{0:T(256)}, f32[256]{0:T(256)S(1)}, u32[]{:S(2)}) copy-start(f32[256]{0:T(256)S(1)} %add_rsqrt_fusion.4) | copy-start | bytes 3076
  218.3 14.8 %copy-start.7 = (bf16[256,256]{0,1:T(8,128)(2,1)S(1)}, bf16[256,256]{0,1:T(8,128)(2,1)}, u32[]{:S(2)}) copy-start(bf16[256,256]{0,1:T(8,128)(2,1)} %copy-done.6) | copy-start | bytes 393220
  241.5 3.1 copy-start.5
  244.7 10.4 %copy-start.8 = (f32[256,2,128]{2,1,0:T(2,128)S(1)}, f32[256,2,128]{2,1,0:T(2,128)}, u32[]{:S(2)}) copy-start(f32[256,2,128]{2,1,0:T(2,128)} %copy.156) | copy-start | bytes 786436
  260.2 7.3 %copy-start.2 = (bf16[256,4096]{1,0:T(8,128)(2,1)S(1)}, bf16[256,4096]{1,0:T(8,128)(2,1)}, u32[]{:S(2)}) copy-start(bf16[256,4096]{1,0:T(8,128)(2,1)} %copy-done.1) | copy-start | bytes 6291460
  260.2 7.3 %copy-start.14 = (f32[1,4096]{1,0:T(1,128)S(1)}, f32[1,4096]{1,0:T(1,128)}, u32[]{:S(2)}) copy-start(f32[1,4096]{1,0:T(1,128)} %get-tuple-element.23) | copy-start | bytes 49156
  260.2 7.2 %copy-start.20 = (f32[256]{0:T(256)S(1)}, f32[256]{0:T(256)}, u32[]{:S(2)}) copy-start(f32[256]{0:T(256)} %copy-done.19) | copy-start | bytes 3076
  260.2 7.2 %copy-start.27 = (f32[256]{0:T(256)S(1)}, f32[256]{0:T(256)}, u32[]{:S(2)}) copy-start(f32[256]{0:T(256)} %copy-done.26) | copy-start | bytes 3076
  297.9 0.9 copy-start.4
  297.9 1.0 copy-start.9
Sparse Core Ops, SparseCore 0:
  122.1 82.5 all-reduce.6
  298.1 79.9 all-reduce.4
where the time goes:
time: 398 us; the launch traced here: 390 us
  matrix products  152 us (38%)
  waiting for transfers between devices  137 us (34%)
  other arithmetic  60.1 us (15%)
  local copies, waits for them, and re-layouts  25.5 us (6%)
  between operations  15.2 us (4%)
    psum x2, waiting for transfers between devices, local_step(): mlp_sum = lax.psum(mlp_part, 'tp')  137 us
    dot_general x2, matrix products, mlp_partial(): jnp.dot(hidden, up_w, preferred_element_type=jnp.float32)  31.2 us
    dot_general x2, matrix products, mlp_partial(): jnp.dot(hidden, gate_w, preferred_element_type=jnp.float32)  29.9 us
    dot_general x2, matrix products, mlp_partial(): return jnp.dot(activated, down_w, preferred_element_type=jnp.float32)  29.6 us
    select_n x1, other arithmetic, write_caches(): v_out = jnp.where(at_pos, jnp.stack(new_values)[:, :, :, None, :], v_cache)  23.3 us
    dot_general x2, matrix products, attend(): jnp.einsum('bkgd,bksd->bkgs', q_grouped, k_old, preferred_element_type=jn...  17 us
    dot_general x4, matrix products, project_heads(): jnp.dot(hidden, weight, preferred_element_type=jnp.float32)  15.7 us
    dot_general x2, matrix products, local_step(): jnp.dot(attn_heads, w_o[layer_idx], preferred_element_type=jnp.float32)  14.3 us
  transfers between devices with their start and end apart: 2, of which 2 were waited for; matrix products, arithmetic and copies ran while one was open for 6% of the time, Pallas kernels for 0%

commit v1 on v0

v1 whole, which is shorter than its diff:
```python
import functools
import math
import jax
import jax.numpy as jnp
from jax import lax
from jax.experimental import pallas as pl
from jax.experimental.pallas import tpu as pltpu
from jax.sharding import PartitionSpec as P

EPS = 1e-5
ROPE_THETA = 75000000.0
F32 = jnp.float32
BF16 = jnp.bfloat16

ROWS = 256
D = 4096
HD = 128
QH = 8
KVH = 2
SEQ = 64
FFL = 3584
QC = QH * HD
ACTC = QC + FFL
TN = 512
NS = 8
GU = 256
N_GU = FFL // GU
CB = 16
N_CB = ROWS // CB
NC = 4
N_OUT = D // TN
HALF = ROWS // 2


def layer_norm(v, w):
    c = v - jnp.mean(v, axis=-1, keepdims=True)
    var = jnp.mean(c * c, axis=-1, keepdims=True)
    return c * lax.rsqrt(var + EPS) * w


def rope(v, cos_b, sin_b):
    even = lax.rem(lax.broadcasted_iota(jnp.int32, v.shape, 1), 2) == 0
    swapped = jnp.where(even, pltpu.roll(v, HD - 1, 1), pltpu.roll(v, 1, 1))
    return v * cos_b + swapped * sin_b


def local_kernel(l, pos_ref, ln_ref, qn_ref, kn_ref, cos_ref, sin_ref, posb_ref, x_hbm, kc, vc, wq, wk, wv, wg, wu, *rest):
    rest = rest[2:] if l else rest
    (act_hbm, k_out, v_out, x_s, h_s, q_s, k_s, v_s, act_s, w_s, kb, vb, x_sem, w_sem, ci_sem, co_sem, act_sem) = rest

    def w_pair(i, slot, a, b, off):
        return (
            pltpu.make_async_copy(a.at[l, :, pl.ds(off, GU)], w_s.at[slot, :, pl.ds(0, GU)], w_sem.at[slot, 0]),
            pltpu.make_async_copy(b.at[l, :, pl.ds(off, GU)], w_s.at[slot, :, pl.ds(GU, GU)], w_sem.at[slot, 1]),
        )

    def tile(i):
        if isinstance(i, int) and i < 2:
            return w_pair(i, i, wq.at[:, :, pl.ds(i * TN, GU)], wq.at[:, :, pl.ds(i * TN + GU, GU)], 0)
        if isinstance(i, int) and i == 2:
            return w_pair(i, i, wk, wv, 0)
        off = (i - 3) * GU
        if not isinstance(i, int):
            off = pl.multiple_of(off, GU)
        return w_pair(i, i % NS if isinstance(i, int) else lax.rem(i, NS), wg, wu, off)

    def start(i):
        for c in tile(i):
            c.start()

    def wait(i):
        for c in tile(i):
            c.wait()

    def cache_in(b, s):
        r = pl.ds(b * CB, CB)
        return (
            pltpu.make_async_copy(kc.at[l, r], kb.at[s], ci_sem.at[s, 0]),
            pltpu.make_async_copy(vc.at[l, r], vb.at[s], ci_sem.at[s, 1]),
        )

    def cache_out(b, s):
        r = pl.ds(b * CB, CB)
        return (
            pltpu.make_async_copy(kb.at[s], k_out.at[l, r], co_sem.at[s, 0]),
            pltpu.make_async_copy(vb.at[s], v_out.at[l, r], co_sem.at[s, 1]),
        )

    x_copy = pltpu.make_async_copy(x_hbm, x_s, x_sem)
    x_copy.start()
    for i in range(3):
        start(i)
    for b in range(NC - 1):
        for c in cache_in(b, b):
            c.start()
    for i in range(3, NS):
        start(i)
    x_copy.wait()

    ln_w = ln_ref[pl.ds(l, 1), :].astype(F32)

    @pl.loop(0, ROWS // 16)
    def _(r):
        rows = pl.ds(pl.multiple_of(r * 16, 16), 16)
        h_s[rows, :] = layer_norm(x_s[rows, :].astype(F32), ln_w).astype(BF16)

    @pl.loop(0, 2)
    def _(t):
        for i in range(2):
            @pl.when(t == i)
            def _():
                wait(i)
        y = jnp.dot(h_s[...], w_s[t], preferred_element_type=F32)
        start(t + NS)
        for j in range(4):
            q_s[t * 4 + j] = y[:, j * HD:(j + 1) * HD]

    wait(2)
    y = jnp.dot(h_s[...], w_s[2], preferred_element_type=F32)
    start(2 + NS)
    for j in range(2):
        k_s[j] = y[:, j * HD:(j + 1) * HD]
        v_s[j] = y[:, GU + j * HD:GU + (j + 1) * HD]

    @pl.loop(0, ROWS // 32)
    def _(r):
        rows = pl.ds(pl.multiple_of(r * 32, 32), 32)
        cb = cos_ref[rows, :]
        sb = sin_ref[rows, :]
        for src, nw, n in ((q_s, qn_ref, QH), (k_s, kn_ref, KVH)):
            for j in range(n):
                v = src[j, rows, :].astype(BF16).astype(F32)
                src[j, rows, :] = rope(layer_norm(v, nw[l, pl.ds(j, 1), :].astype(F32)), cb, sb)

    scale = 1.0 / math.sqrt(HD)
    lane = lax.broadcasted_iota(jnp.int32, (8, 8 * SEQ), 1)
    low = lax.broadcasted_iota(jnp.int32, (8, 8 * SEQ), 0) * SEQ
    sub16 = lax.broadcasted_iota(jnp.int32, (16, HD), 0)

    @pl.loop(0, N_CB)
    def _(b):
        s = lax.rem(b, NC)
        for c in cache_in(b, s):
            c.wait()
        base = pl.multiple_of(b * CB, CB)
        news = [[src[j, pl.ds(base, CB), :] for j in range(KVH)] for src in (k_s, v_s)]
        for r in range(CB):
            p = pos_ref[base + r]
            st = pl.multiple_of((p >> 4) << 4, 16)
            hit = sub16 == p - st
            for buf, new in ((kb, news[0]), (vb, news[1])):
                for j in range(KVH):
                    old = buf[s, r, j, pl.ds(st, 16), :].astype(F32)
                    fresh = jnp.broadcast_to(new[j][r:r + 1, :], (16, HD))
                    buf[s, r, j, pl.ds(st, 16), :] = jnp.where(hit, fresh, old).astype(BF16)
        for j in range(KVH):
            outs = []
            for hf in range(2):
                rows = pl.ds(pl.multiple_of(base + hf * 8, 8), 8)
                q = jnp.concatenate([q_s[j * 4 + g, rows, :] for g in range(4)], axis=0).astype(BF16)
                k = kb[s, hf * 8:(hf + 1) * 8, j].reshape(8 * SEQ, HD)
                sc = lax.dot_general(q, k, (((1,), (1,)), ((), ())), preferred_element_type=F32)
                pb = jnp.concatenate([posb_ref[rows, :]] * 4, axis=1)
                ok = (lane >= low) & (lane <= low + pb)
                probs = []
                for g in range(4):
                    z = jnp.where(ok, sc[g * 8:(g + 1) * 8, :] * scale, -1e30)
                    e = jnp.exp(z - jnp.max(z, axis=-1, keepdims=True))
                    probs.append(e / jnp.sum(e, axis=-1, keepdims=True))
                pr = jnp.concatenate(probs, axis=0).astype(BF16)
                v = vb[s, hf * 8:(hf + 1) * 8, j].reshape(8 * SEQ, HD)
                outs.append(jnp.dot(pr, v, preferred_element_type=F32))
            for g in range(4):
                o = jnp.concatenate([outs[0][g * 8:(g + 1) * 8], outs[1][g * 8:(g + 1) * 8]], axis=0)
                act_s[pl.ds(base, CB), (j * 4 + g) * HD:(j * 4 + g + 1) * HD] = o.astype(BF16)
        for c in cache_out(b, s):
            c.start()

        @pl.when(b + NC - 1 < N_CB)
        def _():
            n = lax.rem(b + NC - 1, NC)

            @pl.when(b >= 1)
            def _():
                for c in cache_out(b - 1, n):
                    c.wait()
            for c in cache_in(b + NC - 1, n):
                c.start()

    def act_copy(t):
        if isinstance(t, int) and t < 0:
            return pltpu.make_async_copy(act_s.at[:, pl.ds(0, QC)], act_hbm.at[:, pl.ds(0, QC)], act_sem.at[N_GU])
        cols = pl.ds(pl.multiple_of(QC + t * GU, GU), GU)
        return pltpu.make_async_copy(act_s.at[:, cols], act_hbm.at[:, cols], act_sem.at[t])

    act_copy(-1).start()

    @pl.loop(0, N_GU)
    def _(t):
        i = t + 3
        wait(i)
        y = jnp.dot(h_s[...], w_s[lax.rem(i, NS)], preferred_element_type=F32)

        @pl.when(i + NS < N_GU + 3)
        def _():
            start(i + NS)
        g = y[:, :GU].astype(BF16).astype(F32)
        u = y[:, GU:].astype(BF16).astype(F32)
        act_s[:, pl.ds(pl.multiple_of(QC + t * GU, GU), GU)] = (g / (1.0 + jnp.exp(-g)) * u).astype(BF16)
        act_copy(t).start()

    act_copy(-1).wait()

    @pl.loop(0, N_GU)
    def _(t):
        act_copy(t).wait()

    for b in range(N_CB - NC, N_CB):
        for c in cache_out(b, b % NC):
            c.wait()


def reduce_kernel(l, act_hbm, x_hbm, wo, wd, out_hbm, act_s, x_s, w_s, part, recv1, send2, recv2, xnew, a_sem, w_sem, s1, r1, s2, r2, s3, r3, o_sem):
    me = lax.axis_index("tp")
    core = lax.rem(me, 2)
    sib = me + 1 - 2 * core
    cross = lax.rem(me + 2, 4)
    own = pl.multiple_of(core * HALF, HALF)
    oth = pl.multiple_of((1 - core) * HALF, HALF)

    def cols(c):
        return pl.ds(c * TN if isinstance(c, int) else pl.multiple_of(c * TN, TN), TN)

    def w_tile(c):
        return (
            pltpu.make_async_copy(wo.at[l, :, cols(c)], w_s.at[c, pl.ds(0, QC), :], w_sem.at[c, 0]),
            pltpu.make_async_copy(wd.at[l, :, cols(c)], w_s.at[c, pl.ds(QC, FFL), :], w_sem.at[c, 1]),
        )

    a_copy = pltpu.make_async_copy(act_hbm, act_s, a_sem.at[0])
    x_copy = pltpu.make_async_copy(x_hbm, x_s, a_sem.at[1])
    a_copy.start()
    for c in range(N_OUT):
        for d in w_tile(c):
            d.start()
    x_copy.start()

    barrier = pltpu.get_barrier_semaphore()
    pl.semaphore_signal(barrier, inc=1, device_id={"tp": sib})
    pl.semaphore_signal(barrier, inc=1, device_id={"tp": cross})
    pl.semaphore_wait(barrier, 2)

    def send_a(c):
        return pltpu.make_async_remote_copy(src_ref=part.at[c, pl.ds(oth, HALF), :], dst_ref=recv1.at[c], send_sem=s1.at[c], recv_sem=r1.at[c], device_id={"tp": sib})

    def send_b(c):
        return pltpu.make_async_remote_copy(src_ref=send2.at[c], dst_ref=recv2.at[c], send_sem=s2.at[c], recv_sem=r2.at[c], device_id={"tp": cross})

    def send_c(c):
        block = xnew.at[pl.ds(own, HALF), cols(c)]
        return pltpu.make_async_remote_copy(src_ref=block, dst_ref=block, send_sem=s3.at[c], recv_sem=r3.at[c], device_id={"tp": sib})

    def step2(c):
        send_a(c).wait_recv()
        send2[c] = (part[c, pl.ds(own, HALF), :].astype(F32) + recv1[c].astype(F32)).astype(BF16)
        send_b(c).start()

    a_copy.wait()

    @pl.loop(0, N_OUT)
    def _(c):
        for d in w_tile(c):
            d.wait()
        part[c] = jnp.dot(act_s[...], w_s[c], preferred_element_type=F32).astype(BF16)
        send_a(c).start()

        @pl.when(c >= 1)
        def _():
            step2(c - 1)

    step2(N_OUT - 1)
    x_copy.wait()

    @pl.loop(0, N_OUT)
    def _(c):
        send_b(c).wait_recv()
        total = send2[c].astype(F32) + recv2[c].astype(F32)
        xnew[pl.ds(own, HALF), cols(c)] = (x_s[pl.ds(own, HALF), cols(c)].astype(F32) + total).astype(BF16)
        send_c(c).start()

    def out_copy(c):
        return pltpu.make_async_copy(xnew.at[:, cols(c)], out_hbm.at[:, cols(c)], o_sem.at[c])

    @pl.loop(0, N_OUT)
    def _(c):
        send_c(c).wait()
        send_a(c).wait_send()
        send_b(c).wait_send()
        out_copy(c).start()

    @pl.loop(0, N_OUT)
    def _(c):
        out_copy(c).wait()


ANY = pl.BlockSpec(memory_space=pl.ANY)
VM = pl.BlockSpec(memory_space=pltpu.VMEM)
SM = pl.BlockSpec(memory_space=pltpu.SMEM)
VLIM = 62 * 1024 * 1024


def local_call(l, tables, x, kc, vc, ws, prev):
    cache = jax.ShapeDtypeStruct(kc.shape, BF16)
    n_in = 15
    return pl.pallas_call(
        functools.partial(local_kernel, l),
        name=f"layer{l}_local",
        out_shape=(jax.ShapeDtypeStruct((ROWS, ACTC), BF16), cache, cache),
        in_specs=[SM] + [VM] * 6 + [ANY] * (8 + len(prev)),
        out_specs=(ANY, ANY, ANY),
        input_output_aliases={n_in: 1, n_in + 1: 2} if prev else {},
        scratch_shapes=[
            pltpu.VMEM((ROWS, D), BF16),
            pltpu.VMEM((ROWS, D), BF16),
            pltpu.VMEM((QH, ROWS, HD), F32),
            pltpu.VMEM((KVH, ROWS, HD), F32),
            pltpu.VMEM((KVH, ROWS, HD), F32),
            pltpu.VMEM((ROWS, ACTC), BF16),
            pltpu.VMEM((NS, D, TN), BF16),
            pltpu.VMEM((NC, CB, KVH, SEQ, HD), BF16),
            pltpu.VMEM((NC, CB, KVH, SEQ, HD), BF16),
            pltpu.SemaphoreType.DMA,
            pltpu.SemaphoreType.DMA((NS, 2)),
            pltpu.SemaphoreType.DMA((NC, 2)),
            pltpu.SemaphoreType.DMA((NC, 2)),
            pltpu.SemaphoreType.DMA((N_GU + 1,)),
        ],
        compiler_params=pltpu.CompilerParams(vmem_limit_bytes=VLIM),
    )(*tables, x, kc, vc, *ws, *prev)


def reduce_call(l, act, x, wo, wd):
    sems = [pltpu.SemaphoreType.DMA((N_OUT,))] * 7
    return pl.pallas_call(
        functools.partial(reduce_kernel, l),
        name=f"layer{l}_reduce",
        out_shape=jax.ShapeDtypeStruct((ROWS, D), BF16),
        in_specs=[ANY] * 4,
        out_specs=ANY,
        scratch_shapes=[
            pltpu.VMEM((ROWS, ACTC), BF16),
            pltpu.VMEM((ROWS, D), BF16),
            pltpu.VMEM((N_OUT, ACTC, TN), BF16),
            pltpu.VMEM((N_OUT, ROWS, TN), BF16),
            pltpu.VMEM((N_OUT, HALF, TN), BF16),
            pltpu.VMEM((N_OUT, HALF, TN), BF16),
            pltpu.VMEM((N_OUT, HALF, TN), BF16),
            pltpu.VMEM((ROWS, D), BF16),
            pltpu.SemaphoreType.DMA((2,)),
            pltpu.SemaphoreType.DMA((N_OUT, 2)),
        ] + sems,
        compiler_params=pltpu.CompilerParams(vmem_limit_bytes=VLIM, collective_id=l, has_side_effects=True),
    )(act, x, wo, wd)


def solution(mesh):
    cache_spec = P(None, "dp", "tp", None, None)
    col_spec = P(None, None, "tp")
    row_spec = P(None, "tp", None)
    resid_spec = P("dp", None)
    in_specs = (resid_spec, P("dp"), cache_spec, cache_spec, P(None, None), col_spec, col_spec, col_spec, row_spec, row_spec, row_spec, col_spec, col_spec, row_spec)
    out_specs = (resid_spec, cache_spec, cache_spec)

    def local_step(residual, positions, k_cache, v_cache, ln_weight, w_q, w_k, w_v, q_norm_w, k_norm_w, w_o, w_gate, w_up, w_down):
        lane = jnp.arange(HD)
        half_ids = (lane // 2).astype(F32)
        inv_freq = ROPE_THETA ** (-2.0 * half_ids / HD)
        angles = positions.astype(F32)[:, None] * inv_freq[None, :]
        cos_b = jnp.cos(angles)
        sin_b = jnp.sin(angles) * jnp.where(lane % 2 == 0, -1.0, 1.0)[None, :]
        pos_b = jnp.broadcast_to(positions[:, None], (ROWS, HD))
        tables = (positions, ln_weight, q_norm_w, k_norm_w, cos_b, sin_b, pos_b)
        ws = (w_q, w_k, w_v, w_gate, w_up)
        x = residual
        prev = ()
        for l in range(2):
            act, *prev = local_call(l, tables, x, k_cache, v_cache, ws, tuple(prev))
            x = reduce_call(l, act, x, w_o, w_down)
        return x, prev[0], prev[1]

    return jax.shard_map(local_step, mesh=mesh, in_specs=in_specs, out_specs=out_specs, check_vma=False)
```

time: 398 us -> 232 us (0.58); the launches traced: 390 us -> 232 us
  Pallas kernels: 0 us -> 224 us
  matrix products: 152 us -> 0 us
  waiting for transfers between devices: 137 us -> 0 us
  other arithmetic: 60.1 us -> 1.93 us
  local copies, waits for them, and re-layouts: 25.5 us -> 4.57 us
  between operations: 15.2 us -> 0.66 us
    pallas_call x0 -> x4, Pallas kernels: none -> 224 us  [the longest x2 141 us: local_call(): pl.pallas_call(functools.partial(local_kernel, l), name=f'layer{l}_local'...]
    dot_general x18 -> x0, matrix products: 152 us -> none  [the longest x2 31.2 us: mlp_partial(): jnp.dot(hidden, up_w, preferred_element_type=jnp.float32)]
    psum x2 -> x0, waiting for transfers between devices: 137 us -> none  [local_step(): mlp_sum = lax.psum(mlp_part, 'tp')]
    select_n x1, other arithmetic: 23.3 us -> 0.01 us  [local_step(): sin_b = jnp.sin(angles) * jnp.where(lane % 2 == 0, -1.0, 1.0)[None, :]]
    reduce_sum x12 -> x0, other arithmetic: 15.8 us -> none  [the longest x4 6.1 us: cohere_norm(): centered = values - jnp.mean(values, axis=-1, keepdims=True)]
    convert_element_type x14 -> x0, local copies, waits for them, and re-layouts: 8.88 us -> none  [the longest x6 4.45 us: project_heads(): projected.reshape(hidden.shape[0], norm_w.shape[0], norm_w.shape[1])]
    another operation x6 -> x0, other arithmetic: 5.5 us -> none
    convert_element_type x4 -> x1, other arithmetic: 5.86 us -> 0.68 us  [local_step(): angles = positions.astype(F32)[:, None] * inv_freq[None, :]]
  transfers between devices with their start and end apart: 2 -> 0, of which waited for: 2 -> 0; matrix products, arithmetic and copies ran while one was open for 6% -> 0% of each run, Pallas kernels for 0% -> 0%
where the time goes in v1:
time: 232 us
  Pallas kernels  224 us (97%)
  local copies, waits for them, and re-layouts  4.57 us (2%)
    pallas_call x2, Pallas kernels, local_call(): pl.pallas_call(functools.partial(local_kernel, l), name=f'layer{l}_local'...  141 us
    pallas_call x2, Pallas kernels, reduce_call(): pl.pallas_call(functools.partial(reduce_kernel, l), name=f'layer{l}_reduc...  83 us

profile of v1, /device:TPU:0, one launch (start us, length us, event | category | flops | bytes accessed | tf_op | source)
XLA Modules:
  0.0 231.6 jit_solution(2717360388852438653)
XLA Ops:
  0.6 0.7 convert_element_type.10
  1.3 1.4 broadcast_in_dim.19.posb_ref
  2.8 1.2 fusion
  4.0 70.6 %layer0_local.1 = (bf16[256,4608]{1,0:T(8,128)(2,1)}, bf16[2,256,2,64,128]{4,3,2,1,0:T(8,128)(2,1)}, bf16[2,256,2,64,128]{4,3,2,1,0:T(8,128)(2,1)}) custom-call(s32[256]{0:T(256)} %pos_ref.3, bf16[2,4096]{1,0:T(2,128)(2,1)} %ln_ref.3, bf16[2,8,128]{2,1,0:T(8,128)(2,1)} %qn_ref.3, bf16[2,2,128]{2,1,0:T(2,128)(2,1)} %kn_ref.3, ...), custom_call_target="tpu_custom_call" | custom-call | tf_op jit(solution)/shard_map/layer0_local/pallas_call | solution.py:315
  74.6 43.2 %layer0_reduce.1.x_hbm = bf16[256,4096]{1,0:T(8,128)(2,1)} custom-call(bf16[256,4608]{1,0:T(8,128)(2,1)} %get-tuple-element.9.act_hbm, bf16[256,4096]{1,0:T(8,128)(2,1)} %x_hbm.3, bf16[2,1024,4096]{2,1,0:T(8,128)(2,1)} %wo.3, bf16[2,3584,4096]{2,1,0:T(8,128)(2,1)} %wd.3), custom_call_target="tpu_custom_call" | custom-call | tf_op jit(solution)/shard_map/layer0_reduce/pallas_call | solution.py:344
  117.8 70.8 %layer1_local.1 = (bf16[256,4608]{1,0:T(8,128)(2,1)}, bf16[2,256,2,64,128]{4,3,2,1,0:T(8,128)(2,1)}, bf16[2,256,2,64,128]{4,3,2,1,0:T(8,128)(2,1)}) custom-call(s32[256]{0:T(256)} %pos_ref.3, bf16[2,4096]{1,0:T(2,128)(2,1)} %ln_ref.3, bf16[2,8,128]{2,1,0:T(8,128)(2,1)} %qn_ref.3, ...), custom_call_target="tpu_custom_call", output_to_operand_aliasing={{1}: (15, {}), {2}: (16, {})} | custom-call | tf_op jit(solution)/shard_map/layer1_local/pallas_call | solution.py:315
  188.6 39.8 %layer1_reduce.1 = bf16[256,4096]{1,0:T(8,128)(2,1)} custom-call(bf16[256,4608]{1,0:T(8,128)(2,1)} %get-tuple-element.12.act_hbm, bf16[256,4096]{1,0:T(8,128)(2,1)} %layer0_reduce.1.x_hbm, bf16[2,1024,4096]{2,1,0:T(8,128)(2,1)} %wo.3, bf16[2,3584,4096]{2,1,0:T(8,128)(2,1)} %wd.3), custom_call_target="tpu_custom_call" | custom-call | tf_op jit(solution)/shard_map/layer1_reduce/pallas_call | solution.py:344
  228.5 3.1 %copy.22 = bf16[256,4096]{1,0:T(8,128)(2,1)} copy(bf16[256,4096]{1,0:T(8,128)(2,1)} %layer1_reduce.1) | data formatting | bytes 4194304
  (1 shorter events, 0.0 us)
